TPU v7x, 256 devices: a whole 4x4x8 slice. The times are simulated.
256 devices in a mesh: tok: 32 (over x, z), head: 8 (over y, core).
Axes of the slice: x: 4, y: 4, z: 8, core: 2. Of those that a mesh axis runs over, the one named last changes fastest.
Arguments:
- queries: bfloat16 [12288, 4096], P('tok', 'head'), may hold values from -100 to 100
- keys: bfloat16 [12288, 1024], P('tok', 'head'), may hold values from -5 to 5
- values: bfloat16 [12288, 1024], P('tok', 'head'), may hold values from -6 to 6
- lengths: int32 [16], replicated, may hold values from 1 to 6144, 12288 in all
- out_weight: bfloat16 [4096, 4096], P('head', 'tok'), may hold values from -0.09375 to 0.09375
Outputs:
- mixed: bfloat16 [12288, 4096], P('tok', 'head')
Inputs may be any that keep to these rules, and one draw needn't show every extreme that they name: Every document has at most 6144 tokens and the lengths sum to 12288.
All inputs are finite; a program needn't handle non-finite values.
Results may differ from a plain program's by a relative error of at most 0.015.
Values may be sent and summed in bfloat16 or wider, within the bound.
A program may use at most 64 MiB of HBM per device.

v0:
```python
import math

import jax
import jax.numpy as jnp
from jax import lax
from jax.sharding import PartitionSpec as P

QH = 32
KVH = 8
HD = 128


def in_one_piece(arrays, axis, dim, along):
    both = jnp.concatenate(arrays, axis=along)
    result, at, done = (lax.all_gather(both, axis, axis=dim, tiled=True), 0, [])
    for a in arrays:
        done.append(lax.slice_in_dim(result, at, at + a.shape[along], axis=along))
        at += a.shape[along]
    return tuple(done)


def doc_index(lengths, positions):
    ends = jnp.cumsum(lengths)
    return jnp.sum((positions[:, None] >= ends[None, :]).astype(jnp.int32), axis=1)


def body(queries, keys, values, lengths, out_weight):
    rows = queries.shape[0]
    groups = keys.shape[1] // HD
    ratio = QH // KVH
    scale = 1.0 / HD**0.5
    mine = lax.axis_index("tok")
    qpos = mine * rows + jnp.arange(rows, dtype=jnp.int32)
    qdoc = doc_index(lengths, qpos)
    qlocal = queries.reshape(rows, groups, ratio, HD)

    def absorb_block(carry, kpiece, vpiece, start):
        running, total, accum = carry
        count = kpiece.shape[0]
        kpos = start + jnp.arange(count, dtype=jnp.int32)
        kdoc = doc_index(lengths, kpos)
        allowed = (
            (qdoc[:, None] == kdoc[None, :])
            & (kpos[None, :] <= qpos[:, None])
            & (kpos[None, :] >= 0)
        )
        scores = (
            jnp.einsum(
                "qgrd,kgd->grqk",
                qlocal,
                kpiece.reshape(count, groups, HD),
                preferred_element_type=jnp.float32,
            )
            * scale
        )
        scores = jnp.where(allowed[None, None], scores, jnp.float32(-1e30))
        newtop = jnp.maximum(running, jnp.max(scores, axis=-1))
        weights = jnp.where(
            allowed[None, None], jnp.exp(scores - newtop[..., None]), jnp.float32(0.0)
        )
        factor = jnp.exp(running - newtop)
        total = total * factor + jnp.sum(weights, axis=-1)
        added = jnp.einsum(
            "grqk,kgd->grqd",
            weights.astype(jnp.bfloat16),
            vpiece.reshape(count, groups, HD),
            preferred_element_type=jnp.float32,
        )
        accum = accum * factor[..., None] + added
        return (newtop, total, accum)

    start_state = (
        jnp.full((groups, ratio, rows), -1e30, jnp.float32),
        jnp.zeros((groups, ratio, rows), jnp.float32),
        jnp.zeros((groups, ratio, rows, HD), jnp.float32),
    )
    kpiece, vpiece = in_one_piece((keys, values), "tok", 0, 1)
    count = kpiece.shape[0]
    width = math.gcd(count, 512)
    turns = count // width

    def one_turn(step, inner):
        offset = step * width
        kpart = lax.dynamic_slice_in_dim(kpiece, offset, width, 0)
        vpart = lax.dynamic_slice_in_dim(vpiece, offset, width, 0)
        return absorb_block(inner, kpart, vpart, offset)

    state = lax.fori_loop(0, turns, one_turn, start_state)
    running, total, accum = state
    result = accum / total[..., None]
    attn = (
        jnp.transpose(result, (2, 0, 1, 3)).reshape(rows, groups * ratio * HD).astype(jnp.bfloat16)
    )
    terms = jnp.dot(
        attn,
        lax.all_gather(out_weight, "tok", axis=1, tiled=True),
        preferred_element_type=jnp.float32,
    )
    return lax.psum_scatter(terms.astype(jnp.bfloat16), "head", scatter_dimension=1, tiled=True)


def solution(mesh):
    placed = (P("tok", "head"), P("tok", "head"), P("tok", "head"), P(), P("head", "tok"))
    return jax.shard_map(
        body, mesh=mesh, in_specs=placed, out_specs=P("tok", "head"), check_vma=False
    )
```

profile of v0, /device:TPU:2, one launch (start us, length us, event | category | flops | bytes accessed | tf_op | source)
XLA Modules:
  0.0 304.7 jit_solution(727397547489880541)
XLA Ops:
  12.1 87.8 %all-gather.3.cloned.1.call-done = bf16[12288,256]{1,0:T(8,128)(2,1)} async-done(((bf16[384,256]{1,0:T(8,128)(2,1)}), bf16[12288,256]{1,0:T(8,128)(2,1)}) %all-gather.3.cloned.1.call-update) | async-done | bytes 6291472 | tf_op jit(solution)/shard_map/all_gather | solution.py:15
  99.9 4.7 %fusion.27 = (bf16[12288,128]{1,0:T(8,128)(2,1)}, bf16[12288,128]{1,0:T(8,128)(2,1)}) fusion(bf16[12288,256]{1,0:T(8,128)(2,1)} %all-gather.3.cloned.1.call-done), kind=kLoop, calls=%fused_computation.38 | loop fusion | bytes 12582912 | tf_op jit(solution)/shard_map/slice | solution.py:17
  104.6 149.5 %while.20 = (s32[]{:T(128)}, f32[1,4,384]{2,1,0:T(4,128)S(1)}, f32[1,4,384]{2,1,0:T(4,128)S(1)}, f32[1,4,384,128]{3,2,1,0:T(8,128)}, s32[384]{0:T(512)S(1)}, /*i...) while((s32[]{:T(128)}, f32[1,4,384]{2,1,0:T(4,128)S(1)}, ...), condition=%wide.region_6.7_spmd.clone, body=%wide.region_2.6_spmd.clone.sunk | while | flops 414288256 | bytes 12566291 | solution.py:88
  112.7 3.2 %fusion.41 = f32[1,4,384,128]{3,2,1,0:T(8,128)} fusion(f32[512,384,4]{1,0,2:T(8,128)S(1)} %get-tuple-element.390, f32[4,384]{1,0:T(4,128)S(1)} %bitcast.85, pred[384,512]{0,1:T(8,128)(4,1)S(1)} %and_and_fusion.2, f32[1,4,384,128]{3,2,1,0:T(8,128)} %get-tuple-element.409, f32[4,384]{1,0:T(4,128)S(1)} %get-tuple-element.391, pred[]{:T(512)S(6)} %compare.3, ...), kind=kOutput, calls=%fused_computation.10.clone.1 | convolution fusion | flops 205848576 | bytes 5058565 | tf_op jit(solution)/shard_map/while/body/eval_jaxpr/grqk,kgd->grqd/dot_general | solution.py:63
  119.0 3.2 %fusion.41 = f32[1,4,384,128]{3,2,1,0:T(8,128)} fusion(f32[512,384,4]{1,0,2:T(8,128)S(1)} %get-tuple-element.390, f32[4,384]{1,0:T(4,128)S(1)} %bitcast.85, pred[384,512]{0,1:T(8,128)(4,1)S(1)} %and_and_fusion.2, f32[1,4,384,128]{3,2,1,0:T(8,128)} %get-tuple-element.409, f32[4,384]{1,0:T(4,128)S(1)} %get-tuple-element.391, pred[]{:T(512)S(6)} %compare.3, ...), kind=kOutput, calls=%fused_computation.10.clone.1 | convolution fusion | flops 205848576 | bytes 5058565 | tf_op jit(solution)/shard_map/while/body/eval_jaxpr/grqk,kgd->grqd/dot_general | solution.py:63
  125.2 3.2 %fusion.41 = f32[1,4,384,128]{3,2,1,0:T(8,128)} fusion(f32[512,384,4]{1,0,2:T(8,128)S(1)} %get-tuple-element.390, f32[4,384]{1,0:T(4,128)S(1)} %bitcast.85, pred[384,512]{0,1:T(8,128)(4,1)S(1)} %and_and_fusion.2, f32[1,4,384,128]{3,2,1,0:T(8,128)} %get-tuple-element.409, f32[4,384]{1,0:T(4,128)S(1)} %get-tuple-element.391, pred[]{:T(512)S(6)} %compare.3, ...), kind=kOutput, calls=%fused_computation.10.clone.1 | convolution fusion | flops 205848576 | bytes 5058565 | tf_op jit(solution)/shard_map/while/body/eval_jaxpr/grqk,kgd->grqd/dot_general | solution.py:63
  131.4 3.2 %fusion.41 = f32[1,4,384,128]{3,2,1,0:T(8,128)} fusion(f32[512,384,4]{1,0,2:T(8,128)S(1)} %get-tuple-element.390, f32[4,384]{1,0:T(4,128)S(1)} %bitcast.85, pred[384,512]{0,1:T(8,128)(4,1)S(1)} %and_and_fusion.2, f32[1,4,384,128]{3,2,1,0:T(8,128)} %get-tuple-element.409, f32[4,384]{1,0:T(4,128)S(1)} %get-tuple-element.391, pred[]{:T(512)S(6)} %compare.3, ...), kind=kOutput, calls=%fused_computation.10.clone.1 | convolution fusion | flops 205848576 | bytes 5058565 | tf_op jit(solution)/shard_map/while/body/eval_jaxpr/grqk,kgd->grqd/dot_general | solution.py:63
  143.9 3.2 %fusion.41 = f32[1,4,384,128]{3,2,1,0:T(8,128)} fusion(f32[512,384,4]{1,0,2:T(8,128)S(1)} %get-tuple-element.390, f32[4,384]{1,0:T(4,128)S(1)} %bitcast.85, pred[384,512]{0,1:T(8,128)(4,1)S(1)} %and_and_fusion.2, f32[1,4,384,128]{3,2,1,0:T(8,128)} %get-tuple-element.409, f32[4,384]{1,0:T(4,128)S(1)} %get-tuple-element.391, pred[]{:T(512)S(6)} %compare.3, ...), kind=kOutput, calls=%fused_computation.10.clone.1 | convolution fusion | flops 205848576 | bytes 5058565 | tf_op jit(solution)/shard_map/while/body/eval_jaxpr/grqk,kgd->grqd/dot_general | solution.py:63
  150.2 3.2 %fusion.41 = f32[1,4,384,128]{3,2,1,0:T(8,128)} fusion(f32[512,384,4]{1,0,2:T(8,128)S(1)} %get-tuple-element.390, f32[4,384]{1,0:T(4,128)S(1)} %bitcast.85, pred[384,512]{0,1:T(8,128)(4,1)S(1)} %and_and_fusion.2, f32[1,4,384,128]{3,2,1,0:T(8,128)} %get-tuple-element.409, f32[4,384]{1,0:T(4,128)S(1)} %get-tuple-element.391, pred[]{:T(512)S(6)} %compare.3, ...), kind=kOutput, calls=%fused_computation.10.clone.1 | convolution fusion | flops 205848576 | bytes 5058565 | tf_op jit(solution)/shard_map/while/body/eval_jaxpr/grqk,kgd->grqd/dot_general | solution.py:63
  156.4 3.3 %fusion.41 = f32[1,4,384,128]{3,2,1,0:T(8,128)} fusion(f32[512,384,4]{1,0,2:T(8,128)S(1)} %get-tuple-element.390, f32[4,384]{1,0:T(4,128)S(1)} %bitcast.85, pred[384,512]{0,1:T(8,128)(4,1)S(1)} %and_and_fusion.2, f32[1,4,384,128]{3,2,1,0:T(8,128)} %get-tuple-element.409, f32[4,384]{1,0:T(4,128)S(1)} %get-tuple-element.391, pred[]{:T(512)S(6)} %compare.3, ...), kind=kOutput, calls=%fused_computation.10.clone.1 | convolution fusion | flops 205848576 | bytes 5058565 | tf_op jit(solution)/shard_map/while/body/eval_jaxpr/grqk,kgd->grqd/dot_general | solution.py:63
  162.7 3.2 %fusion.41 = f32[1,4,384,128]{3,2,1,0:T(8,128)} fusion(f32[512,384,4]{1,0,2:T(8,128)S(1)} %get-tuple-element.390, f32[4,384]{1,0:T(4,128)S(1)} %bitcast.85, pred[384,512]{0,1:T(8,128)(4,1)S(1)} %and_and_fusion.2, f32[1,4,384,128]{3,2,1,0:T(8,128)} %get-tuple-element.409, f32[4,384]{1,0:T(4,128)S(1)} %get-tuple-element.391, pred[]{:T(512)S(6)} %compare.3, ...), kind=kOutput, calls=%fused_computation.10.clone.1 | convolution fusion | flops 205848576 | bytes 5058565 | tf_op jit(solution)/shard_map/while/body/eval_jaxpr/grqk,kgd->grqd/dot_general | solution.py:63
  168.9 3.2 %fusion.41 = f32[1,4,384,128]{3,2,1,0:T(8,128)} fusion(f32[512,384,4]{1,0,2:T(8,128)S(1)} %get-tuple-element.390, f32[4,384]{1,0:T(4,128)S(1)} %bitcast.85, pred[384,512]{0,1:T(8,128)(4,1)S(1)} %and_and_fusion.2, f32[1,4,384,128]{3,2,1,0:T(8,128)} %get-tuple-element.409, f32[4,384]{1,0:T(4,128)S(1)} %get-tuple-element.391, pred[]{:T(512)S(6)} %compare.3, ...), kind=kOutput, calls=%fused_computation.10.clone.1 | convolution fusion | flops 205848576 | bytes 5058565 | tf_op jit(solution)/shard_map/while/body/eval_jaxpr/grqk,kgd->grqd/dot_general | solution.py:63
  175.2 3.2 %fusion.41 = f32[1,4,384,128]{3,2,1,0:T(8,128)} fusion(f32[512,384,4]{1,0,2:T(8,128)S(1)} %get-tuple-element.390, f32[4,384]{1,0:T(4,128)S(1)} %bitcast.85, pred[384,512]{0,1:T(8,128)(4,1)S(1)} %and_and_fusion.2, f32[1,4,384,128]{3,2,1,0:T(8,128)} %get-tuple-element.409, f32[4,384]{1,0:T(4,128)S(1)} %get-tuple-element.391, pred[]{:T(512)S(6)} %compare.3, ...), kind=kOutput, calls=%fused_computation.10.clone.1 | convolution fusion | flops 205848576 | bytes 5058565 | tf_op jit(solution)/shard_map/while/body/eval_jaxpr/grqk,kgd->grqd/dot_general | solution.py:63
  181.4 3.2 %fusion.41 = f32[1,4,384,128]{3,2,1,0:T(8,128)} fusion(f32[512,384,4]{1,0,2:T(8,128)S(1)} %get-tuple-element.390, f32[4,384]{1,0:T(4,128)S(1)} %bitcast.85, pred[384,512]{0,1:T(8,128)(4,1)S(1)} %and_and_fusion.2, f32[1,4,384,128]{3,2,1,0:T(8,128)} %get-tuple-element.409, f32[4,384]{1,0:T(4,128)S(1)} %get-tuple-element.391, pred[]{:T(512)S(6)} %compare.3, ...), kind=kOutput, calls=%fused_computation.10.clone.1 | convolution fusion | flops 205848576 | bytes 5058565 | tf_op jit(solution)/shard_map/while/body/eval_jaxpr/grqk,kgd->grqd/dot_general | solution.py:63
  187.7 3.2 %fusion.41 = f32[1,4,384,128]{3,2,1,0:T(8,128)} fusion(f32[512,384,4]{1,0,2:T(8,128)S(1)} %get-tuple-element.390, f32[4,384]{1,0:T(4,128)S(1)} %bitcast.85, pred[384,512]{0,1:T(8,128)(4,1)S(1)} %and_and_fusion.2, f32[1,4,384,128]{3,2,1,0:T(8,128)} %get-tuple-element.409, f32[4,384]{1,0:T(4,128)S(1)} %get-tuple-element.391, pred[]{:T(512)S(6)} %compare.3, ...), kind=kOutput, calls=%fused_computation.10.clone.1 | convolution fusion | flops 205848576 | bytes 5058565 | tf_op jit(solution)/shard_map/while/body/eval_jaxpr/grqk,kgd->grqd/dot_general | solution.py:63
  193.9 3.2 %fusion.41 = f32[1,4,384,128]{3,2,1,0:T(8,128)} fusion(f32[512,384,4]{1,0,2:T(8,128)S(1)} %get-tuple-element.390, f32[4,384]{1,0:T(4,128)S(1)} %bitcast.85, pred[384,512]{0,1:T(8,128)(4,1)S(1)} %and_and_fusion.2, f32[1,4,384,128]{3,2,1,0:T(8,128)} %get-tuple-element.409, f32[4,384]{1,0:T(4,128)S(1)} %get-tuple-element.391, pred[]{:T(512)S(6)} %compare.3, ...), kind=kOutput, calls=%fused_computation.10.clone.1 | convolution fusion | flops 205848576 | bytes 5058565 | tf_op jit(solution)/shard_map/while/body/eval_jaxpr/grqk,kgd->grqd/dot_general | solution.py:63
  200.1 3.2 %fusion.41 = f32[1,4,384,128]{3,2,1,0:T(8,128)} fusion(f32[512,384,4]{1,0,2:T(8,128)S(1)} %get-tuple-element.390, f32[4,384]{1,0:T(4,128)S(1)} %bitcast.85, pred[384,512]{0,1:T(8,128)(4,1)S(1)} %and_and_fusion.2, f32[1,4,384,128]{3,2,1,0:T(8,128)} %get-tuple-element.409, f32[4,384]{1,0:T(4,128)S(1)} %get-tuple-element.391, pred[]{:T(512)S(6)} %compare.3, ...), kind=kOutput, calls=%fused_computation.10.clone.1 | convolution fusion | flops 205848576 | bytes 5058565 | tf_op jit(solution)/shard_map/while/body/eval_jaxpr/grqk,kgd->grqd/dot_general | solution.py:63
  206.4 3.2 %fusion.41 = f32[1,4,384,128]{3,2,1,0:T(8,128)} fusion(f32[512,384,4]{1,0,2:T(8,128)S(1)} %get-tuple-element.390, f32[4,384]{1,0:T(4,128)S(1)} %bitcast.85, pred[384,512]{0,1:T(8,128)(4,1)S(1)} %and_and_fusion.2, f32[1,4,384,128]{3,2,1,0:T(8,128)} %get-tuple-element.409, f32[4,384]{1,0:T(4,128)S(1)} %get-tuple-element.391, pred[]{:T(512)S(6)} %compare.3, ...), kind=kOutput, calls=%fused_computation.10.clone.1 | convolution fusion | flops 205848576 | bytes 5058565 | tf_op jit(solution)/shard_map/while/body/eval_jaxpr/grqk,kgd->grqd/dot_general | solution.py:63
  218.8 3.2 %fusion.41 = f32[1,4,384,128]{3,2,1,0:T(8,128)} fusion(f32[512,384,4]{1,0,2:T(8,128)S(1)} %get-tuple-element.390, f32[4,384]{1,0:T(4,128)S(1)} %bitcast.85, pred[384,512]{0,1:T(8,128)(4,1)S(1)} %and_and_fusion.2, f32[1,4,384,128]{3,2,1,0:T(8,128)} %get-tuple-element.409, f32[4,384]{1,0:T(4,128)S(1)} %get-tuple-element.391, pred[]{:T(512)S(6)} %compare.3, ...), kind=kOutput, calls=%fused_computation.10.clone.1 | convolution fusion | flops 205848576 | bytes 5058565 | tf_op jit(solution)/shard_map/while/body/eval_jaxpr/grqk,kgd->grqd/dot_general | solution.py:63
  231.3 3.2 %fusion.41 = f32[1,4,384,128]{3,2,1,0:T(8,128)} fusion(f32[512,384,4]{1,0,2:T(8,128)S(1)} %get-tuple-element.390, f32[4,384]{1,0:T(4,128)S(1)} %bitcast.85, pred[384,512]{0,1:T(8,128)(4,1)S(1)} %and_and_fusion.2, f32[1,4,384,128]{3,2,1,0:T(8,128)} %get-tuple-element.409, f32[4,384]{1,0:T(4,128)S(1)} %get-tuple-element.391, pred[]{:T(512)S(6)} %compare.3, ...), kind=kOutput, calls=%fused_computation.10.clone.1 | convolution fusion | flops 205848576 | bytes 5058565 | tf_op jit(solution)/shard_map/while/body/eval_jaxpr/grqk,kgd->grqd/dot_general | solution.py:63
  243.8 3.2 %fusion.41 = f32[1,4,384,128]{3,2,1,0:T(8,128)} fusion(f32[512,384,4]{1,0,2:T(8,128)S(1)} %get-tuple-element.390, f32[4,384]{1,0:T(4,128)S(1)} %bitcast.85, pred[384,512]{0,1:T(8,128)(4,1)S(1)} %and_and_fusion.2, f32[1,4,384,128]{3,2,1,0:T(8,128)} %get-tuple-element.409, f32[4,384]{1,0:T(4,128)S(1)} %get-tuple-element.391, pred[]{:T(512)S(6)} %compare.3, ...), kind=kOutput, calls=%fused_computation.10.clone.1 | convolution fusion | flops 205848576 | bytes 5058565 | tf_op jit(solution)/shard_map/while/body/eval_jaxpr/grqk,kgd->grqd/dot_general | solution.py:63
  250.0 3.2 %fusion.41 = f32[1,4,384,128]{3,2,1,0:T(8,128)} fusion(f32[512,384,4]{1,0,2:T(8,128)S(1)} %get-tuple-element.390, f32[4,384]{1,0:T(4,128)S(1)} %bitcast.85, pred[384,512]{0,1:T(8,128)(4,1)S(1)} %and_and_fusion.2, f32[1,4,384,128]{3,2,1,0:T(8,128)} %get-tuple-element.409, f32[4,384]{1,0:T(4,128)S(1)} %get-tuple-element.391, pred[]{:T(512)S(6)} %compare.3, ...), kind=kOutput, calls=%fused_computation.10.clone.1 | convolution fusion | flops 205848576 | bytes 5058565 | tf_op jit(solution)/shard_map/while/body/eval_jaxpr/grqk,kgd->grqd/dot_general | solution.py:63
  255.6 5.7 %convolution_convert_fusion = bf16[384,4096]{1,0:T(8,128)(2,1)} fusion(bf16[384,512]{0,1:T(8,128)(2,1)S(1)} %bitcast.88, bf16[512,4096]{1,0:T(8,128)(2,1)} %all-gather.5.cloned.1.call-done), kind=kOutput, calls=%fused_computation.33 | convolution fusion | flops 1612185600 | bytes 7733248 | tf_op jit(solution)/shard_map/dot_general | solution.py:94
  261.3 36.9 %reduce-scatter.2.cloned.1.call-done = bf16[384,512]{1,0:T(8,128)(2,1)} async-done(((bf16[384,4096]{1,0:T(8,128)(2,1)}), bf16[384,512]{1,0:T(8,128)(2,1)}) %reduce-scatter.2.cloned.1.call-update) | async-done | bytes 393232 | tf_op jit(solution)/shard_map/reduce_scatter | solution.py:99
  (263 shorter events, 93.3 us)
Async XLA Ops:
  6.5 93.4 %all-gather.3.cloned.1.call-start = ((), (), s32[]{:S(2)}) async-start(), calls=%async_computation.1 | async-start | bytes 6488064 | tf_op jit(solution)/shard_map/all_gather | solution.py:15
  8.2 247.4 %all-gather.5.cloned.1.call-start = ((), (), s32[]{:S(2)}) async-start(), calls=%async_computation.2 | async-start | bytes 4325376 | tf_op jit(solution)/shard_map/all_gather | solution.py:96
  9.0 289.2 %reduce-scatter.2.cloned.1.call-start = ((), (), s32[]{:S(2)}) async-start(), calls=%async_computation.3 | async-start | bytes 3538944 | tf_op jit(solution)/shard_map/reduce_scatter | solution.py:99
Sparse Core Ops, SparseCore 0:
  9.9 89.9 all-gather.2
  102.4 81.1 all-gather.4
  261.4 36.6 reduce-scatter.1
where the time goes:
time: 306 us; the launch traced here: 305 us
  waiting for transfers between devices  125 us (41%)
  matrix products  125 us (41%)
  other arithmetic  31.2 us (10%)
  between operations  13.2 us (4%)
  local copies, waits for them, and re-layouts  8.28 us (3%)
    all_gather x1, waiting for transfers between devices, in_one_piece(): result, at, done = (lax.all_gather(both, axis, axis=dim, tiled=True), 0, [])  87.8 us
    dot_general x24, matrix products, absorb_block(): jnp.einsum('grqk,kgd->grqd', weights.astype(jnp.bfloat16), vpiece.reshape...  77.2 us
    dot_general x24, matrix products, absorb_block(): jnp.einsum('qgrd,kgd->grqk', qlocal, kpiece.reshape(count, groups, HD), p...  41.9 us
    reduce_scatter x1, waiting for transfers between devices, body(): lax.psum_scatter(terms.astype(jnp.bfloat16), 'head', scatter_dimension=1,...  36.9 us
    reduce_sum x24, other arithmetic, absorb_block(): total = total * factor + jnp.sum(weights, axis=-1)  18.8 us
    and x24, other arithmetic, absorb_block(): (qdoc[:, None] == kdoc[None, :]) & (kpos[None, :] <= qpos[:, None])  6.59 us
  transfers between devices with their start and end apart: 3, of which 2 were waited for; matrix products, arithmetic and copies ran while one was open for 52% of the time, Pallas kernels for 0%

commit v1 on v0

v1 whole, which is shorter than its diff:
```python
import functools
import math

import jax
import jax.numpy as jnp
from jax import lax
from jax.experimental import pallas as pl
from jax.experimental.pallas import tpu as pltpu
from jax.sharding import PartitionSpec as P

HD = 128
NX, NZ, NY = 4, 8, 4
MESH = pl.DeviceIdType.MESH
FAR = -1e30
BF = jnp.bfloat16
F32 = jnp.float32


def kernel(
    scale,
    q_hbm, k_hbm, v_hbm, w_hbm, len_ref, o_ref,
    q, kv, wa, wb, start, top, total, accum, attn, mid, give, take, up, down, rup, rdown, tup, tdown,
    load, kv_recv, zp, zm, xs,
    axs, axr, azps, azpr, azms, azmr, bzps, bzpr, bzms, bzmr, bxs, bxr,
    gs, gr, rs, rr,
):
    tok = lax.axis_index("tok")
    head = lax.axis_index("head")
    x, z = lax.div(tok, NZ), lax.rem(tok, NZ)
    y, core = lax.div(head, 2), lax.rem(head, 2)
    rows = q.shape[0]
    ratio = q.shape[1] // HD
    ha = wa.shape[2]

    def at_xz(xx, zz):
        return {"tok": lax.rem(xx + NX, NX) * NZ + lax.rem(zz + NZ, NZ), "head": head}

    def at_y(yy, cc):
        return {"tok": tok, "head": lax.rem(yy + NY, NY) * 2 + cc}

    def remote(src, dst, send, recv, dev):
        return pltpu.make_async_remote_copy(
            src_ref=src, dst_ref=dst, send_sem=send, recv_sem=recv,
            device_id=dev, device_id_type=MESH,
        )

    east, west, south = at_xz(x + 1, z), at_xz(x + 3, z), at_xz(x + 2, z)
    zup, zdown = at_xz(x, z + 1), at_xz(x, z + 7)
    pair = at_y(y, 1 - core)
    yup, ydown = at_y(y + 1, core), at_y(y + 3, core)

    loads = [
        pltpu.make_async_copy(k_hbm, kv.at[0, z, 0], load.at[0]),
        pltpu.make_async_copy(v_hbm, kv.at[0, z, 1], load.at[1]),
        pltpu.make_async_copy(w_hbm.at[pl.ds(0, ha)], wa.at[z, x], load.at[2]),
        pltpu.make_async_copy(w_hbm.at[pl.ds(ha, wb.shape[2])], wb.at[x, z], load.at[3]),
        pltpu.make_async_copy(q_hbm, q, load.at[4]),
    ]
    for c in loads:
        c.start()

    barrier = pltpu.get_barrier_semaphore()
    greeted = (east, west, south, zup, zdown, pair, yup, ydown)
    for dev in greeted:
        pl.semaphore_signal(barrier, inc=1, device_id=dev, device_id_type=MESH)
    pl.semaphore_wait(barrier, len(greeted))

    def kv_zup(zz):
        return remote(kv.at[0, zz], kv.at[0, zz], zp.at[zz], kv_recv.at[0, zz], zup)

    def kv_zdown(zz):
        return remote(kv.at[1, zz], kv.at[1, zz], zm.at[zz], kv_recv.at[1, zz], zdown)

    def kv_east(t, zz, k):
        return remote(kv.at[t, zz], kv.at[t + 1, zz], xs.at[k], kv_recv.at[t + 1, zz], east)

    def kv_arrive(t, zz):
        remote(kv.at[t, zz], kv.at[t, zz], zp.at[0], kv_recv.at[t, zz], east).wait_recv()

    def item(k):
        na, nb = z + 1, NZ - z
        m = jnp.minimum(na, nb)
        both = k < 2 * m
        kind = jnp.where(both, lax.rem(k, 2), jnp.where(na > nb, 0, 1))
        j = jnp.where(both, lax.div(k, 2), k - m)
        return kind, jnp.where(kind == 0, z - j, z + j)

    def ax(d):
        return remote(wa.at[z, x], wa.at[z, x], axs.at[d - 1], axr.at[d - 1], at_xz(x + d, z))

    def azp(s):
        b = wa.at[lax.rem(z + NZ - s, NZ)]
        return remote(b, b, azps.at[s], azpr.at[s], zup)

    def azm(s):
        b = wa.at[lax.rem(z + s, NZ)]
        return remote(b, b, azms.at[s], azmr.at[s], zdown)

    def bzp(s):
        b = wb.at[x, lax.rem(z + NZ - s, NZ)]
        return remote(b, b, bzps.at[s], bzpr.at[s], zup)

    def bzm(s):
        b = wb.at[x, lax.rem(z + s, NZ)]
        return remote(b, b, bzms.at[s], bzmr.at[s], zdown)

    def bx(s):
        b = wb.at[lax.rem(x + s, NX)]
        return remote(b, b, bxs.at[s], bxr.at[s], west)

    last_up, last_down = lax.rem(z + 1, NZ) < 4, lax.rem(z + 7, NZ) >= 4
    get_up, get_down = z < 4, z >= 4

    loads[0].wait()
    loads[1].wait()

    @pl.when(z < NZ - 1)
    def _():
        kv_zup(z).start()

    @pl.when(x < NX - 1)
    def _():
        kv_east(0, z, 0).start()

    loads[2].wait()
    loads[3].wait()
    for d in (1, 2, 3):
        ax(d).start()
    bzp(0).start()
    bzm(0).start()
    loads[4].wait()

    qpos = tok * rows + lax.broadcasted_iota(jnp.int32, (rows, HD), 0)
    edge = jnp.int32(0)
    first = jnp.zeros((rows, HD), jnp.int32)
    for d in range(len_ref.shape[0]):
        edge = edge + len_ref[d]
        first = jnp.maximum(first, jnp.where(qpos >= edge, edge, 0))
    start[...] = first

    lane = lax.broadcasted_iota(jnp.int32, (rows, HD), 1)
    tiles = rows // HD

    def attend(t, zz, fresh):
        base = ((x - t) * NZ + zz) * rows
        kblock = kv[t, zz, 0]
        vblock = kv[t, zz, 1]
        near = start[...] - base
        allowed = []
        for j in range(tiles):
            ok = lane + j * HD >= near
            if fresh:
                ok = ok & (lane + j * HD <= lax.broadcasted_iota(jnp.int32, (rows, HD), 0))
            allowed.append(ok)
        for r in range(ratio):
            s = lax.dot_general(
                q[:, r * HD : (r + 1) * HD], kblock, (((1,), (1,)), ((), ())),
                preferred_element_type=F32,
            )
            parts = [
                jnp.where(allowed[j], s[:, j * HD : (j + 1) * HD], FAR) for j in range(tiles)
            ]
            peak = jnp.max(functools.reduce(jnp.maximum, parts), axis=1, keepdims=True)
            if fresh:
                new = jnp.broadcast_to(peak, (rows, HD))
            else:
                old = top[r]
                new = jnp.maximum(old, peak)
                fade = jnp.exp2((old - new) * scale)
            weights = [jnp.exp2((p - new) * scale) for p in parts]
            added = functools.reduce(jnp.add, weights)
            low = jnp.concatenate([w.astype(BF) for w in weights], axis=1)
            gain = jnp.dot(low, vblock, preferred_element_type=F32)
            top[r] = new
            if fresh:
                total[r] = added
                accum[r] = gain
            else:
                total[r] = total[r] * fade + added
                accum[r] = accum[r] * fade + gain

    attend(0, z, True)

    def step(k, carry):
        have_a = k <= z
        have_b = (x > 0) & (z + k - 1 < NZ)
        az, bz = z - k, z + k - 1

        @pl.when(have_a)
        def _():
            kv_arrive(0, az)

        @pl.when(have_a & (z < NZ - 1))
        def _():
            kv_zup(az).start()

        @pl.when(have_b)
        def _():
            kv_arrive(1, bz)

        @pl.when(have_b & (z > 0))
        def _():
            kv_zdown(bz).start()

        kind, zz = item(k)

        @pl.when((k <= NZ) & (x < NX - 1) & ((kind == 0) | (x > 0)))
        def _():
            kv_east(kind, zz, k).start()

        @pl.when(k == 1)
        def _():
            bzp(0).wait_recv()
            bzp(1).start()
            bzm(0).wait_recv()
            bzm(1).start()
            for d in (1, 2, 3):
                ax(d).wait_recv()
            azp(0).start()
            azm(0).start()

        @pl.when(k == 2)
        def _():
            bzp(1).wait_recv()
            bzp(2).start()
            bzm(1).wait_recv()
            bzm(2).start()

        @pl.when(k == 3)
        def _():
            bzp(2).wait_recv()
            bzm(2).wait_recv()
            azp(0).wait_recv()
            azp(1).start()
            azm(0).wait_recv()
            azm(1).start()

        @pl.when((k == 3) & last_up)
        def _():
            bzp(3).start()

        @pl.when((k == 3) & last_down)
        def _():
            bzm(3).start()

        @pl.when((k == 4) & get_up)
        def _():
            bzp(3).wait_recv()

        @pl.when((k == 4) & get_down)
        def _():
            bzm(3).wait_recv()

        @pl.when(k == 4)
        def _():
            bx(0).start()

        @pl.when(k == 5)
        def _():
            azp(1).wait_recv()
            azp(2).start()
            azm(1).wait_recv()
            azm(2).start()

        @pl.when(k == 7)
        def _():
            azp(2).wait_recv()
            azm(2).wait_recv()
            bx(0).wait_recv()
            bx(1).start()

        @pl.when((k == 7) & last_up)
        def _():
            azp(3).start()

        @pl.when((k == 7) & last_down)
        def _():
            azm(3).start()

        @pl.when(k == 9)
        def _():
            bx(1).wait_recv()
            bx(2).start()

        @pl.when(have_a)
        def _():
            attend(0, az, False)

        @pl.when(have_b)
        def _():
            attend(1, bz, False)

        kind, zz = item(k - 1)
        have_x = (k > 1) & (x > 0) & ((kind == 0) | (x > 1))

        @pl.when(have_x)
        def _():
            kv_arrive(kind + 1, zz)
            attend(kind + 1, zz, False)

        return carry

    lax.fori_loop(1, NZ + 2, step, 0)

    for r in range(ratio):
        whole = jnp.sum(total[r], axis=1, keepdims=True)
        attn[:, r * HD : (r + 1) * HD] = (accum[r] / whole).astype(BF)

    bx(2).wait_recv()

    @pl.when(get_up)
    def _():
        azp(3).wait_recv()

    @pl.when(get_down)
    def _():
        azm(3).wait_recv()

    def project(g, c):
        out = []
        for h in (0, 2):
            zz = c * 4 + h
            ra = jnp.concatenate([wa[zz, g], wa[zz + 1, g]], axis=1)
            rb = jnp.concatenate([wb[g, zz], wb[g, zz + 1]], axis=1)
            out.append(
                jnp.dot(attn[:, :ha], ra, preferred_element_type=F32)
                + jnp.dot(attn[:, ha:], rb, preferred_element_type=F32)
            )
        return jnp.concatenate(out, axis=1)

    def swap(i):
        return remote(give.at[i], take.at[i], gs.at[i], gr.at[i], pair)

    half = rows // 2
    lo, hi = pl.ds(0, half), pl.ds(half, half)
    targets = [lax.rem(y + d, NY) for d in (2, 1, 3, 0)]

    def first_pass(i, carry):
        g = lax.rem(y + jnp.where(i == 0, 2, jnp.where(i == 1, 1, jnp.where(i == 2, 3, 0))), NY)
        give[i] = project(g, 1 - core).astype(BF)
        swap(i).start()
        return carry

    lax.fori_loop(0, NY, first_pass, 0)

    far_up = remote(mid.at[lo], rup, rs.at[0], rr.at[0], yup)
    far_down = remote(mid.at[hi], rdown, rs.at[1], rr.at[1], ydown)
    up_hi = remote(up.at[hi], tup.at[hi], rs.at[2], rr.at[2], yup)
    down_lo = remote(down.at[lo], tdown.at[lo], rs.at[3], rr.at[3], ydown)
    up_lo = remote(up.at[lo], tup.at[lo], rs.at[4], rr.at[4], yup)
    down_hi = remote(down.at[hi], tdown.at[hi], rs.at[5], rr.at[5], ydown)

    def both_cores(i):
        mine = project(targets[i], core)
        swap(i).wait_recv()
        return mine + take[i].astype(F32)

    mid[...] = both_cores(0).astype(BF)
    far_up.start()
    far_down.start()
    part = both_cores(1)
    up[hi] = part[half:].astype(BF)
    accum_up = part[:half]
    up_hi.start()
    part = both_cores(2)
    down[lo] = part[:half].astype(BF)
    accum_down = part[half:]
    down_lo.start()
    far_up.wait_recv()
    up[lo] = (accum_up + rup[...].astype(F32)).astype(BF)
    up_lo.start()
    far_down.wait_recv()
    down[hi] = (accum_down + rdown[...].astype(F32)).astype(BF)
    down_hi.start()
    mine = both_cores(3)
    up_hi.wait_recv()
    down_lo.wait_recv()
    up_lo.wait_recv()
    down_hi.wait_recv()
    o_ref[...] = (mine + tup[...].astype(F32) + tdown[...].astype(F32)).astype(BF)

    for i in range(NY):
        swap(i).wait_send()
    for c in (far_up, far_down, up_hi, down_lo, up_lo, down_hi):
        c.wait_send()
    for d in (1, 2, 3):
        ax(d).wait_send()
    for s in range(3):
        for c in (azp(s), azm(s), bzp(s), bzm(s), bx(s)):
            c.wait_send()

    @pl.when(last_up)
    def _():
        azp(3).wait_send()
        bzp(3).wait_send()

    @pl.when(last_down)
    def _():
        azm(3).wait_send()
        bzm(3).wait_send()

    def drain(k, carry):
        @pl.when((k <= z) & (z < NZ - 1))
        def _():
            kv_zup(k).wait_send()

        @pl.when((k >= z) & (z > 0) & (x > 0) & (k < NZ))
        def _():
            kv_zdown(k).wait_send()

        kind, zz = item(k)

        @pl.when((x < NX - 1) & ((kind == 0) | (x > 0)))
        def _():
            kv_east(kind, zz, k).wait_send()

        return carry

    lax.fori_loop(0, NZ + 1, drain, 0)


def body(queries, keys, values, lengths, out_weight):
    rows, width = queries.shape
    depth = out_weight.shape[0]
    ha = depth // 2
    scale = math.log2(math.e) / math.sqrt(HD)
    ratio = width // HD
    dma = pltpu.SemaphoreType.DMA
    any_ = pl.BlockSpec(memory_space=pl.ANY)
    return pl.pallas_call(
        functools.partial(kernel, scale),
        out_shape=jax.ShapeDtypeStruct((rows, width), BF),
        in_specs=[any_, any_, any_, any_, pl.BlockSpec(memory_space=pltpu.SMEM)],
        out_specs=pl.BlockSpec(memory_space=pltpu.VMEM),
        scratch_shapes=[
            pltpu.VMEM((rows, width), BF),
            pltpu.VMEM((3, NZ, 2, rows, HD), BF),
            pltpu.VMEM((NZ, NX, ha, HD), BF),
            pltpu.VMEM((NX, NZ, depth - ha, HD), BF),
            pltpu.VMEM((rows, HD), jnp.int32),
            pltpu.VMEM((ratio, rows, HD), F32),
            pltpu.VMEM((ratio, rows, HD), F32),
            pltpu.VMEM((ratio, rows, HD), F32),
            pltpu.VMEM((rows, width), BF),
            pltpu.VMEM((rows, width), BF),
            pltpu.VMEM((NY, rows, width), BF),
            pltpu.VMEM((NY, rows, width), BF),
            pltpu.VMEM((rows, width), BF),
            pltpu.VMEM((rows, width), BF),
            pltpu.VMEM((rows // 2, width), BF),
            pltpu.VMEM((rows // 2, width), BF),
            pltpu.VMEM((rows, width), BF),
            pltpu.VMEM((rows, width), BF),
            dma((5,)), dma((3, NZ)), dma((NZ,)), dma((NZ,)), dma((NZ + 1,)),
            dma((3,)), dma((3,)),
            dma((4,)), dma((4,)), dma((4,)), dma((4,)),
            dma((4,)), dma((4,)), dma((4,)), dma((4,)),
            dma((3,)), dma((3,)),
            dma((NY,)), dma((NY,)), dma((6,)), dma((6,)),
        ],
        compiler_params=pltpu.CompilerParams(
            collective_id=0, has_side_effects=True, vmem_limit_bytes=60 * 1024 * 1024
        ),
    )(queries, keys, values, out_weight, lengths)


def solution(mesh):
    placed = (P("tok", "head"), P("tok", "head"), P("tok", "head"), P(), P("head", "tok"))
    return jax.shard_map(
        body, mesh=mesh, in_specs=placed, out_specs=P("tok", "head"), check_vma=False
    )
```

time: 306 us -> 104 us (0.34)
  matrix products: 125 us -> 0 us
  waiting for transfers between devices: 125 us -> 0 us
  Pallas kernels: 0 us -> 102 us
  other arithmetic: 31.2 us -> 0 us
  between operations: 13.2 us -> 0.01 us
  local copies, waits for them, and re-layouts: 8.28 us -> 1.77 us
    dot_general x49 -> x0, matrix products: 125 us -> none  [the longest x24 77.2 us: absorb_block(): jnp.einsum('grqk,kgd->grqd', weights.astype(jnp.bfloat16), vpiece.reshape...]
    pallas_call x0 -> x1, Pallas kernels: none -> 102 us  [body(): pl.pallas_call(functools.partial(kernel, scale), out_shape=jax.ShapeDtype...]
    all_gather x2 -> x0, waiting for transfers between devices: 87.8 us -> none  [the longest x1 87.8 us: in_one_piece(): result, at, done = (lax.all_gather(both, axis, axis=dim, tiled=True), 0, [])]
    reduce_scatter x1 -> x0, waiting for transfers between devices: 36.9 us -> none  [body(): lax.psum_scatter(terms.astype(jnp.bfloat16), 'head', scatter_dimension=1,...]
    reduce_sum x49 -> x0, other arithmetic: 21 us -> none  [the longest x24 18.8 us: absorb_block(): total = total * factor + jnp.sum(weights, axis=-1)]
    and x24 -> x0, other arithmetic: 6.59 us -> none  [absorb_block(): (qdoc[:, None] == kdoc[None, :]) & (kpos[None, :] <= qpos[:, None])]
    slice x1 -> x0, local copies, waits for them, and re-layouts: 4.69 us -> none  [in_one_piece(): done.append(lax.slice_in_dim(result, at, at + a.shape[along], axis=along))]
  transfers between devices with their start and end apart: 3 -> 0, of which waited for: 2 -> 0; matrix products, arithmetic and copies ran while one was open for 52% -> 0% of each run, Pallas kernels for 0% -> 0%
where the time goes in v1:
time: 104 us
  Pallas kernels  102 us (98%)
  local copies, waits for them, and re-layouts  1.77 us (2%)
    pallas_call x1, Pallas kernels, body(): pl.pallas_call(functools.partial(kernel, scale), out_shape=jax.ShapeDtype...  102 us

profile of v1, /device:TPU:2, one launch (start us, length us, event | category | flops | bytes accessed | tf_op | source)
XLA Modules:
  0.0 104.0 jit_solution(4010037259909074797)
XLA Ops:
  0.0 102.2 %shard_map.55 = bf16[384,512]{1,0:T(8,128)(2,1)} custom-call(bf16[384,512]{1,0:T(8,128)(2,1)} %q_hbm.1, bf16[384,128]{1,0:T(8,128)(2,1)} %k_hbm.1, bf16[384,128]{1,0:T(8,128)(2,1)} %v_hbm.1, bf16[512,128]{1,0:T(8,128)(2,1)} %w_hbm.1, s32[16]{0:T(128)} %len_ref.1), custom_call_target="tpu_custom_call" | custom-call | tf_op jit(solution)/shard_map/pallas_call | solution.py:430
  102.3 1.8 %copy.7 = bf16[384,512]{1,0:T(8,128)(2,1)} copy(bf16[384,512]{1,0:T(8,128)(2,1)} %shard_map.55) | data formatting | bytes 786432

commit v2 on v1

--- a/solution.py
+++ b/solution.py
@@ -14,6 +14,16 @@
 FAR = -1e30
 BF = jnp.bfloat16
 F32 = jnp.float32
+PLAN = {
+    1: ((0, 1), (2, 0, 1), (2, 0, 2)),
+    2: ((0, 2), (2, 0, 3), (2, 0, 4), (2, 1, 0)),
+    3: ((0, 3), (2, 0, 5), (2, 0, 6), (2, 1, 1), (1, 0)),
+    4: ((0, 4), (2, 0, 7), (2, 1, 2), (2, 1, 3)),
+    5: ((2, 1, 4), (2, 1, 5), (2, 2, 0), (1, 1)),
+    6: ((2, 1, 6), (2, 1, 7), (2, 2, 1), (1, 2)),
+    7: ((2, 2, 2), (2, 2, 3), (2, 2, 4)),
+    8: ((2, 2, 5), (2, 2, 6), (2, 2, 7), (1, 3)),
+}
 
 
 def kernel(
@@ -65,17 +75,22 @@
         pl.semaphore_signal(barrier, inc=1, device_id=dev, device_id_type=MESH)
     pl.semaphore_wait(barrier, len(greeted))
 
-    def kv_zup(zz):
-        return remote(kv.at[0, zz], kv.at[0, zz], zp.at[zz], kv_recv.at[0, zz], zup)
-
-    def kv_zdown(zz):
-        return remote(kv.at[1, zz], kv.at[1, zz], zm.at[zz], kv_recv.at[1, zz], zdown)
-
-    def kv_east(t, zz, k):
-        return remote(kv.at[t, zz], kv.at[t + 1, zz], xs.at[k], kv_recv.at[t + 1, zz], east)
-
-    def kv_arrive(t, zz):
-        remote(kv.at[t, zz], kv.at[t, zz], zp.at[0], kv_recv.at[t, zz], east).wait_recv()
+    def kv_zup(zz, p):
+        b = kv.at[0, zz, p]
+        return remote(b, b, zp.at[zz, p], kv_recv.at[0, zz, p], zup)
+
+    def kv_zdown(zz, p):
+        b = kv.at[1, zz, p]
+        return remote(b, b, zm.at[zz, p], kv_recv.at[1, zz, p], zdown)
+
+    def kv_east(t, zz, k, p):
+        return remote(
+            kv.at[t, zz, p], kv.at[t + 1, zz, p], xs.at[k, p], kv_recv.at[t + 1, zz, p], east
+        )
+
+    def kv_arrive(t, zz, p):
+        b = kv.at[t, zz, p]
+        remote(b, b, zp.at[0, p], kv_recv.at[t, zz, p], east).wait_recv()
 
     def item(k):
         na, nb = z + 1, NZ - z
@@ -104,30 +119,74 @@
         b = wb.at[x, lax.rem(z + s, NZ)]
         return remote(b, b, bzms.at[s], bzmr.at[s], zdown)
 
-    def bx(s):
-        b = wb.at[lax.rem(x + s, NX)]
-        return remote(b, b, bxs.at[s], bxr.at[s], west)
+    order = (0, 1, 7, 2, 6, 3, 5, 4)
+
+    def bx(d, i):
+        b = wb.at[lax.rem(x + d, NX), lax.rem(z + order[i], NZ)]
+        return remote(b, b, bxs.at[d, i], bxr.at[d, i], west)
 
     last_up, last_down = lax.rem(z + 1, NZ) < 4, lax.rem(z + 7, NZ) >= 4
     get_up, get_down = z < 4, z >= 4
 
-    loads[0].wait()
-    loads[1].wait()
-
-    @pl.when(z < NZ - 1)
-    def _():
-        kv_zup(z).start()
-
-    @pl.when(x < NX - 1)
-    def _():
-        kv_east(0, z, 0).start()
-
+    def hop(up, down, s):
+        if s == 4:
+
+            @pl.when(get_up)
+            def _():
+                up(3).wait_recv()
+
+            @pl.when(get_down)
+            def _():
+                down(3).wait_recv()
+
+            return
+        if s:
+            up(s - 1).wait_recv()
+            down(s - 1).wait_recv()
+        if s < 3:
+            up(s).start()
+            down(s).start()
+        else:
+
+            @pl.when(last_up)
+            def _():
+                up(3).start()
+
+            @pl.when(last_down)
+            def _():
+                down(3).start()
+
+    def relay(kind, s, i=0):
+        if kind == 0:
+            hop(bzp, bzm, s)
+        elif kind == 1:
+            if s == 0:
+                for d in (1, 2, 3):
+                    ax(d).wait_recv()
+            hop(azp, azm, s)
+        else:
+            if s:
+                bx(s - 1, i).wait_recv()
+            bx(s, i).start()
+
+    for p in (0, 1):
+        loads[p].wait()
+
+        @pl.when(z < NZ - 1)
+        def _():
+            kv_zup(z, p).start()
+
+        @pl.when(x < NX - 1)
+        def _():
+            kv_east(0, z, 0, p).start()
+
+    loads[3].wait()
+    bzp(0).start()
+    bzm(0).start()
+    bx(0, 0).start()
     loads[2].wait()
-    loads[3].wait()
     for d in (1, 2, 3):
         ax(d).start()
-    bzp(0).start()
-    bzm(0).start()
     loads[4].wait()
 
     qpos = tok * rows + lax.broadcasted_iota(jnp.int32, (rows, HD), 0)
@@ -186,101 +245,36 @@
         have_b = (x > 0) & (z + k - 1 < NZ)
         az, bz = z - k, z + k - 1
 
-        @pl.when(have_a)
-        def _():
-            kv_arrive(0, az)
-
-        @pl.when(have_a & (z < NZ - 1))
-        def _():
-            kv_zup(az).start()
-
-        @pl.when(have_b)
-        def _():
-            kv_arrive(1, bz)
-
-        @pl.when(have_b & (z > 0))
-        def _():
-            kv_zdown(bz).start()
-
         kind, zz = item(k)
-
-        @pl.when((k <= NZ) & (x < NX - 1) & ((kind == 0) | (x > 0)))
-        def _():
-            kv_east(kind, zz, k).start()
-
-        @pl.when(k == 1)
-        def _():
-            bzp(0).wait_recv()
-            bzp(1).start()
-            bzm(0).wait_recv()
-            bzm(1).start()
-            for d in (1, 2, 3):
-                ax(d).wait_recv()
-            azp(0).start()
-            azm(0).start()
-
-        @pl.when(k == 2)
-        def _():
-            bzp(1).wait_recv()
-            bzp(2).start()
-            bzm(1).wait_recv()
-            bzm(2).start()
-
-        @pl.when(k == 3)
-        def _():
-            bzp(2).wait_recv()
-            bzm(2).wait_recv()
-            azp(0).wait_recv()
-            azp(1).start()
-            azm(0).wait_recv()
-            azm(1).start()
-
-        @pl.when((k == 3) & last_up)
-        def _():
-            bzp(3).start()
-
-        @pl.when((k == 3) & last_down)
-        def _():
-            bzm(3).start()
-
-        @pl.when((k == 4) & get_up)
-        def _():
-            bzp(3).wait_recv()
-
-        @pl.when((k == 4) & get_down)
-        def _():
-            bzm(3).wait_recv()
-
-        @pl.when(k == 4)
-        def _():
-            bx(0).start()
-
-        @pl.when(k == 5)
-        def _():
-            azp(1).wait_recv()
-            azp(2).start()
-            azm(1).wait_recv()
-            azm(2).start()
-
-        @pl.when(k == 7)
-        def _():
-            azp(2).wait_recv()
-            azm(2).wait_recv()
-            bx(0).wait_recv()
-            bx(1).start()
-
-        @pl.when((k == 7) & last_up)
-        def _():
-            azp(3).start()
-
-        @pl.when((k == 7) & last_down)
-        def _():
-            azm(3).start()
-
-        @pl.when(k == 9)
-        def _():
-            bx(1).wait_recv()
-            bx(2).start()
+        have_item = (k <= NZ) & (x < NX - 1) & ((kind == 0) | (x > 0))
+        for p in (0, 1):
+
+            @pl.when(have_a)
+            def _():
+                kv_arrive(0, az, p)
+
+            @pl.when(have_a & (z < NZ - 1))
+            def _():
+                kv_zup(az, p).start()
+
+            @pl.when(have_b)
+            def _():
+                kv_arrive(1, bz, p)
+
+            @pl.when(have_b & (z > 0))
+            def _():
+                kv_zdown(bz, p).start()
+
+            @pl.when(have_item)
+            def _():
+                kv_east(kind, zz, k, p).start()
+
+        for when, moves in PLAN.items():
+
+            @pl.when(k == when)
+            def _():
+                for move in moves:
+                    relay(*move)
 
         @pl.when(have_a)
         def _():
@@ -295,7 +289,8 @@
 
         @pl.when(have_x)
         def _():
-            kv_arrive(kind + 1, zz)
+            kv_arrive(kind + 1, zz, 0)
+            kv_arrive(kind + 1, zz, 1)
             attend(kind + 1, zz, False)
 
         return carry
@@ -306,15 +301,9 @@
         whole = jnp.sum(total[r], axis=1, keepdims=True)
         attn[:, r * HD : (r + 1) * HD] = (accum[r] / whole).astype(BF)
 
-    bx(2).wait_recv()
-
-    @pl.when(get_up)
-    def _():
-        azp(3).wait_recv()
-
-    @pl.when(get_down)
-    def _():
-        azm(3).wait_recv()
+    for i in range(NZ):
+        bx(2, i).wait_recv()
+    hop(azp, azm, 4)
 
     def project(g, c):
         out = []
@@ -386,7 +375,7 @@
     for d in (1, 2, 3):
         ax(d).wait_send()
     for s in range(3):
-        for c in (azp(s), azm(s), bzp(s), bzm(s), bx(s)):
+        for c in (azp(s), azm(s), bzp(s), bzm(s), *(bx(s, i) for i in range(NZ))):
             c.wait_send()
 
     @pl.when(last_up)
@@ -402,17 +391,20 @@
     def drain(k, carry):
         @pl.when((k <= z) & (z < NZ - 1))
         def _():
-            kv_zup(k).wait_send()
+            kv_zup(k, 0).wait_send()
+            kv_zup(k, 1).wait_send()
 
         @pl.when((k >= z) & (z > 0) & (x > 0) & (k < NZ))
         def _():
-            kv_zdown(k).wait_send()
+            kv_zdown(k, 0).wait_send()
+            kv_zdown(k, 1).wait_send()
 
         kind, zz = item(k)
 
         @pl.when((x < NX - 1) & ((kind == 0) | (x > 0)))
         def _():
-            kv_east(kind, zz, k).wait_send()
+            kv_east(kind, zz, k, 0).wait_send()
+            kv_east(kind, zz, k, 1).wait_send()
 
         return carry
 
@@ -422,7 +414,7 @@
 def body(queries, keys, values, lengths, out_weight):
     rows, width = queries.shape
     depth = out_weight.shape[0]
-    ha = depth // 2
+    ha = depth * 3 // 8
     scale = math.log2(math.e) / math.sqrt(HD)
     ratio = width // HD
     dma = pltpu.SemaphoreType.DMA
@@ -451,11 +443,11 @@
             pltpu.VMEM((rows // 2, width), BF),
             pltpu.VMEM((rows, width), BF),
             pltpu.VMEM((rows, width), BF),
-            dma((5,)), dma((3, NZ)), dma((NZ,)), dma((NZ,)), dma((NZ + 1,)),
+            dma((5,)), dma((3, NZ, 2)), dma((NZ, 2)), dma((NZ, 2)), dma((NZ + 1, 2)),
             dma((3,)), dma((3,)),
             dma((4,)), dma((4,)), dma((4,)), dma((4,)),
             dma((4,)), dma((4,)), dma((4,)), dma((4,)),
-            dma((3,)), dma((3,)),
+            dma((3, NZ)), dma((3, NZ)),
             dma((NY,)), dma((NY,)), dma((6,)), dma((6,)),
         ],
         compiler_params=pltpu.CompilerParams(

time: 104 us -> 87.5 us (0.84)
  Pallas kernels: 102 us -> 85.5 us
    pallas_call x1, Pallas kernels: 102 us -> 85.5 us  [body(): pl.pallas_call(functools.partial(kernel, scale), out_shape=jax.ShapeDtype...]
where the time goes in v2:
time: 87.5 us; the launch traced here: 87.3 us
  Pallas kernels  85.5 us (98%)
  local copies, waits for them, and re-layouts  1.77 us (2%)
    pallas_call x1, Pallas kernels, body(): pl.pallas_call(functools.partial(kernel, scale), out_shape=jax.ShapeDtype...  85.5 us
    unnamed x1, local copies, waits for them, and re-layouts  1.77 us

profile of v2, /device:TPU:2, one launch (start us, length us, event | category | flops | bytes accessed | tf_op | source)
XLA Modules:
  0.0 87.3 jit_solution(11847688736355926363)
XLA Ops:
  0.0 85.5 %shard_map.55 = bf16[384,512]{1,0:T(8,128)(2,1)} custom-call(bf16[384,512]{1,0:T(8,128)(2,1)} %q_hbm.1, bf16[384,128]{1,0:T(8,128)(2,1)} %k_hbm.1, bf16[384,128]{1,0:T(8,128)(2,1)} %v_hbm.1, bf16[512,128]{1,0:T(8,128)(2,1)} %w_hbm.1, s32[16]{0:T(128)} %len_ref.1), custom_call_target="tpu_custom_call" | custom-call | tf_op jit(solution)/shard_map/pallas_call | solution.py:422
  85.5 1.8 %copy.7 = bf16[384,512]{1,0:T(8,128)(2,1)} copy(bf16[384,512]{1,0:T(8,128)(2,1)} %shard_map.55) | data formatting | bytes 786432

commit v3 on v2

--- a/solution.py
+++ b/solution.py
@@ -100,6 +100,14 @@
         j = jnp.where(both, lax.div(k, 2), k - m)
         return kind, jnp.where(kind == 0, z - j, z + j)
 
+    def kv_first(p):
+        b = kv.at[0, 0, p]
+        return remote(b, b, zm.at[0, p], kv_recv.at[0, 0, p], zdown)
+
+    def kv_last(p):
+        b = kv.at[1, NZ - 1, p]
+        return remote(b, b, zp.at[NZ - 1, p], kv_recv.at[1, NZ - 1, p], zup)
+
     def ax(d):
         return remote(wa.at[z, x], wa.at[z, x], axs.at[d - 1], axr.at[d - 1], at_xz(x + d, z))
 
@@ -175,6 +183,10 @@
         @pl.when(z < NZ - 1)
         def _():
             kv_zup(z, p).start()
+
+        @pl.when(z == 0)
+        def _():
+            kv_first(p).start()
 
         @pl.when(x < NX - 1)
         def _():
@@ -242,7 +254,8 @@
 
     def step(k, carry):
         have_a = k <= z
-        have_b = (x > 0) & (z + k - 1 < NZ)
+        have_b = (x > 0) & (z + k - 1 < NZ) & ((z > 0) | (k < NZ))
+        have_r = (x > 0) & (z == 0) & (k == 2)
         az, bz = z - k, z + k - 1
 
         kind, zz = item(k)
@@ -253,7 +266,7 @@
             def _():
                 kv_arrive(0, az, p)
 
-            @pl.when(have_a & (z < NZ - 1))
+            @pl.when(have_a & (z < NZ - 1) & ((z < NZ - 2) | (az > 0)))
             def _():
                 kv_zup(az, p).start()
 
@@ -261,9 +274,17 @@
             def _():
                 kv_arrive(1, bz, p)
 
-            @pl.when(have_b & (z > 0))
+            @pl.when(have_b & (z > 0) & ((z > 1) | (bz < NZ - 1)))
             def _():
                 kv_zdown(bz, p).start()
+
+            @pl.when((k == 1) & (x > 0) & (z == NZ - 1))
+            def _():
+                kv_last(p).start()
+
+            @pl.when(have_r)
+            def _():
+                kv_arrive(1, NZ - 1, p)
 
             @pl.when(have_item)
             def _():
@@ -283,6 +304,10 @@
         @pl.when(have_b)
         def _():
             attend(1, bz, False)
+
+        @pl.when(have_r)
+        def _():
+            attend(1, NZ - 1, False)
 
         kind, zz = item(k - 1)
         have_x = (k > 1) & (x > 0) & ((kind == 0) | (x > 1))
@@ -389,15 +414,25 @@
         bzm(3).wait_send()
 
     def drain(k, carry):
-        @pl.when((k <= z) & (z < NZ - 1))
-        def _():
-            kv_zup(k, 0).wait_send()
-            kv_zup(k, 1).wait_send()
-
-        @pl.when((k >= z) & (z > 0) & (x > 0) & (k < NZ))
-        def _():
-            kv_zdown(k, 0).wait_send()
-            kv_zdown(k, 1).wait_send()
+        @pl.when((k <= z) & (z < NZ - 1) & ((z < NZ - 2) | (k > 0)))
+        def _():
+            for p in (0, 1):
+                kv_zup(k, p).wait_send()
+
+        @pl.when((k >= z) & (z > 0) & (x > 0) & (k < NZ) & ((z > 1) | (k < NZ - 1)))
+        def _():
+            for p in (0, 1):
+                kv_zdown(k, p).wait_send()
+
+        @pl.when((k == 0) & (z == 0))
+        def _():
+            for p in (0, 1):
+                kv_first(p).wait_send()
+
+        @pl.when((k == 0) & (x > 0) & (z == NZ - 1))
+        def _():
+            for p in (0, 1):
+                kv_last(p).wait_send()
 
         kind, zz = item(k)
 

time: 87.5 us -> 84.9 us (0.970)
  Pallas kernels: 85.5 us -> 83 us
    pallas_call x1, Pallas kernels: 85.5 us -> 83 us  [body(): pl.pallas_call(functools.partial(kernel, scale), out_shape=jax.ShapeDtype...]
where the time goes in v3:
time: 84.9 us; the launch traced here: 84.8 us
  Pallas kernels  83 us (98%)
  local copies, waits for them, and re-layouts  1.77 us (2%)
    pallas_call x1, Pallas kernels, body(): pl.pallas_call(functools.partial(kernel, scale), out_shape=jax.ShapeDtype...  83 us
    unnamed x1, local copies, waits for them, and re-layouts  1.77 us

profile of v3, /device:TPU:2, one launch (start us, length us, event | category | flops | bytes accessed | tf_op | source)
XLA Modules:
  0.0 84.8 jit_solution(16625608358901343024)
XLA Ops:
  0.0 83.0 %shard_map.55 = bf16[384,512]{1,0:T(8,128)(2,1)} custom-call(bf16[384,512]{1,0:T(8,128)(2,1)} %q_hbm.1, bf16[384,128]{1,0:T(8,128)(2,1)} %k_hbm.1, bf16[384,128]{1,0:T(8,128)(2,1)} %v_hbm.1, bf16[512,128]{1,0:T(8,128)(2,1)} %w_hbm.1, s32[16]{0:T(128)} %len_ref.1), custom_call_target="tpu_custom_call" | custom-call | tf_op jit(solution)/shard_map/pallas_call | solution.py:457
  83.0 1.8 %copy.7 = bf16[384,512]{1,0:T(8,128)(2,1)} copy(bf16[384,512]{1,0:T(8,128)(2,1)} %shard_map.55) | data formatting | bytes 786432

commit v4 on v3

--- a/solution.py
+++ b/solution.py
@@ -15,14 +15,14 @@
 BF = jnp.bfloat16
 F32 = jnp.float32
 PLAN = {
-    1: ((0, 1), (2, 0, 1), (2, 0, 2)),
-    2: ((0, 2), (2, 0, 3), (2, 0, 4), (2, 1, 0)),
-    3: ((0, 3), (2, 0, 5), (2, 0, 6), (2, 1, 1), (1, 0)),
-    4: ((0, 4), (2, 0, 7), (2, 1, 2), (2, 1, 3)),
-    5: ((2, 1, 4), (2, 1, 5), (2, 2, 0), (1, 1)),
-    6: ((2, 1, 6), (2, 1, 7), (2, 2, 1), (1, 2)),
-    7: ((2, 2, 2), (2, 2, 3), (2, 2, 4)),
-    8: ((2, 2, 5), (2, 2, 6), (2, 2, 7), (1, 3)),
+    1: ((0, 1), (2, 0, 1), (2, 0, 2), (2, 1, 0)),
+    2: ((0, 2), (2, 0, 3), (2, 0, 4), (2, 1, 1), (2, 1, 2), (1, 0)),
+    3: ((0, 3), (2, 0, 5), (2, 1, 3), (2, 1, 4), (2, 2, 1)),
+    4: ((0, 4), (2, 0, 6), (2, 1, 5), (1, 1)),
+    5: ((2, 0, 7), (2, 1, 6), (2, 2, 2), (2, 2, 4), (2, 2, 5)),
+    6: ((1, 2),),
+    7: ((2, 1, 7), (2, 2, 0)),
+    8: ((2, 2, 3), (2, 2, 6), (2, 2, 7), (1, 3)),
 }
 
 
@@ -449,7 +449,7 @@
 def body(queries, keys, values, lengths, out_weight):
     rows, width = queries.shape
     depth = out_weight.shape[0]
-    ha = depth * 3 // 8
+    ha = depth * 11 // 32
     scale = math.log2(math.e) / math.sqrt(HD)
     ratio = width // HD
     dma = pltpu.SemaphoreType.DMA

time: 84.9 us -> 84.3 us (level)
  Pallas kernels: 83 us -> 82.1 us
    pallas_call x1, Pallas kernels: 83 us -> 82.1 us  [body(): pl.pallas_call(functools.partial(kernel, scale), out_shape=jax.ShapeDtype...]
where the time goes in v4:
time: 84.3 us; the launch traced here: 83.9 us
  Pallas kernels  82.1 us (97%)
  local copies, waits for them, and re-layouts  1.77 us (2%)
    pallas_call x1, Pallas kernels, body(): pl.pallas_call(functools.partial(kernel, scale), out_shape=jax.ShapeDtype...  82.1 us
    unnamed x1, local copies, waits for them, and re-layouts  1.77 us

profile of v4, /device:TPU:2, one launch (start us, length us, event | category | flops | bytes accessed | tf_op | source)
XLA Modules:
  0.0 83.9 jit_solution(17746423078779978925)
XLA Ops:
  0.0 82.1 %shard_map.55 = bf16[384,512]{1,0:T(8,128)(2,1)} custom-call(bf16[384,512]{1,0:T(8,128)(2,1)} %q_hbm.1, bf16[384,128]{1,0:T(8,128)(2,1)} %k_hbm.1, bf16[384,128]{1,0:T(8,128)(2,1)} %v_hbm.1, bf16[512,128]{1,0:T(8,128)(2,1)} %w_hbm.1, s32[16]{0:T(128)} %len_ref.1), custom_call_target="tpu_custom_call" | custom-call | tf_op jit(solution)/shard_map/pallas_call | solution.py:457
  82.1 1.8 %copy.7 = bf16[384,512]{1,0:T(8,128)(2,1)} copy(bf16[384,512]{1,0:T(8,128)(2,1)} %shard_map.55) | data formatting | bytes 786432

commit v5 on v4

--- a/solution.py
+++ b/solution.py
@@ -334,12 +334,10 @@
         out = []
         for h in (0, 2):
             zz = c * 4 + h
-            ra = jnp.concatenate([wa[zz, g], wa[zz + 1, g]], axis=1)
-            rb = jnp.concatenate([wb[g, zz], wb[g, zz + 1]], axis=1)
-            out.append(
-                jnp.dot(attn[:, :ha], ra, preferred_element_type=F32)
-                + jnp.dot(attn[:, ha:], rb, preferred_element_type=F32)
-            )
+            left = jnp.concatenate([wa[zz, g], wb[g, zz]], axis=0)
+            right = jnp.concatenate([wa[zz + 1, g], wb[g, zz + 1]], axis=0)
+            both = jnp.concatenate([left, right], axis=1)
+            out.append(jnp.dot(attn[...], both, preferred_element_type=F32))
         return jnp.concatenate(out, axis=1)
 
     def swap(i):

time: 84.3 us -> 84.2 us (level)
  no operation moved by 1% of the time
where the time goes in v5:
time: 84.2 us; the launch traced here: 83.8 us
  Pallas kernels  82 us (97%)
  local copies, waits for them, and re-layouts  1.77 us (2%)
    pallas_call x1, Pallas kernels, body(): pl.pallas_call(functools.partial(kernel, scale), out_shape=jax.ShapeDtype...  82 us
    unnamed x1, local copies, waits for them, and re-layouts  1.77 us

profile of v5, /device:TPU:2, one launch (start us, length us, event | category | flops | bytes accessed | tf_op | source)
XLA Modules:
  0.0 83.8 jit_solution(6859740797542281941)
XLA Ops:
  0.0 82.0 %shard_map.55 = bf16[384,512]{1,0:T(8,128)(2,1)} custom-call(bf16[384,512]{1,0:T(8,128)(2,1)} %q_hbm.1, bf16[384,128]{1,0:T(8,128)(2,1)} %k_hbm.1, bf16[384,128]{1,0:T(8,128)(2,1)} %v_hbm.1, bf16[512,128]{1,0:T(8,128)(2,1)} %w_hbm.1, s32[16]{0:T(128)} %len_ref.1), custom_call_target="tpu_custom_call" | custom-call | tf_op jit(solution)/shard_map/pallas_call | solution.py:455
  82.0 1.8 %copy.7 = bf16[384,512]{1,0:T(8,128)(2,1)} copy(bf16[384,512]{1,0:T(8,128)(2,1)} %shard_map.55) | data formatting | bytes 786432
